TPU v7x, 32 devices: a 4x2x2 block of a 4x4x8 slice. The times are simulated.
32 devices in a mesh: dp: 4 (over y, z), tp: 8 (over x, core).
Axes of the slice: x: 4, y: 2, z: 2, core: 2. Of those that a mesh axis runs over, the one named last changes fastest.
The devices are a block of a 4x4x8 slice.
Arguments:
- token_ids: int32 [4, 8192], P('dp'), parts along dimension 0
- emb_table: bfloat16 [32000, 2048], P('tp')
- norm_gain: bfloat16 [2048], replicated
- grad_out: bfloat16 [4, 8192, 2048], P('dp', 'tp'), parts along dimension 0
Outputs:
- output 1: bfloat16 [4, 8192, 2048], P('dp', 'tp'), parts along dimension 0
- output 2: float32 [128000, 2048], P(('dp', 'tp')), parts along dimension 0
- output 3: float32 [8192], P('dp'), parts along dimension 0
There are 4 independent parts. A program takes and returns all parts, laid end to end along the dimension named above; an argument that names none is the same for every part.
All inputs are finite; a program needn't handle non-finite values.
Results may differ from a plain program's by a relative error of at most 0.00852753.
Values are sent between devices in bfloat16 or wider.
A program may use at most 768 MiB of HBM per device.

v0:
```python
import jax
import jax.numpy as jnp
from jax import lax
from jax.sharding import PartitionSpec as P

RMS_EPS = 1e-5


def norm_pass(embedded, norm_gain, grad_block):
    hidden_f32 = embedded.astype(jnp.float32)
    inv_rms = lax.rsqrt(jnp.mean(hidden_f32 * hidden_f32, axis=-1, keepdims=True) + RMS_EPS)
    x_hat = hidden_f32 * inv_rms
    normed = x_hat.astype(jnp.bfloat16) * norm_gain
    grad_f32 = grad_block.astype(jnp.float32)
    gain_part = jnp.sum(grad_f32 * x_hat, axis=(0, 1))
    grad_hat = grad_f32 * norm_gain.astype(jnp.float32)
    grad_in = (inv_rms * (grad_hat - x_hat * jnp.mean(grad_hat * x_hat, axis=-1, keepdims=True))).astype(jnp.bfloat16)
    return normed, grad_in, gain_part


def device_step(token_ids, table_block, norm_gain, grad_block):
    rows_block, hidden_size = table_block.shape
    tp_index = lax.axis_index('tp')
    local_ids = token_ids - tp_index * rows_block
    owned = (local_ids >= 0) & (local_ids < rows_block)
    looked_up = jnp.take(table_block, jnp.where(owned, local_ids, 0), axis=0)
    partial_rows = jnp.where(owned[:, :, None], looked_up, jnp.zeros((), jnp.bfloat16))
    embedded = lax.psum_scatter(partial_rows, 'tp', scatter_dimension=1, tiled=True)
    normed, grad_in, gain_part = norm_pass(embedded, norm_gain, grad_block)
    grad_gain = lax.psum(gain_part, 'tp')
    grad_all = lax.all_gather(grad_in, 'tp', axis=1, tiled=True)
    segment_ids = jnp.where(owned, local_ids, rows_block).reshape(-1)
    grad_table = jax.ops.segment_sum(grad_all.astype(jnp.float32).reshape(-1, hidden_size), segment_ids, num_segments=rows_block)
    return normed, grad_table, grad_gain


def solution(mesh):
    return jax.shard_map(device_step, mesh=mesh, in_specs=(P('dp', None), P('tp', None), P(None), P('dp', 'tp', None)), out_specs=(P('dp', 'tp', None), P(('dp', 'tp'), None), P('dp')), check_vma=False)
```

profile of v0, /device:TPU:81, one launch (start us, length us, event | category | flops | bytes accessed | tf_op | source)
XLA Modules:
  0.0 564.4 jit_solution(8077393361578749820)
XLA Ops:
  7.2 0.1 reduce-scatter.2.cloned.1.call-start
  7.2 1.0 and_reduce_fusion
  8.3 69.1 %gather_fusion = bf16[8192,2048]{1,0:T(8,128)(2,1)} fusion(bf16[4000,2048]{1,0:T(8,128)(2,1)} %param.5, s32[8192]{0:T(1024)S(1)} %broadcast_clamp_fusion), kind=kCustom, calls=%fused_computation | custom fusion | bytes 67141632 | tf_op jit(solution)/shard_map/jit(_take)/gather | solution.py:26
  77.4 23.1 %fusion.3 = bf16[1,8192,2048]{2,1,0:T(8,128)(2,1)} fusion(bf16[8192,2048]{1,0:T(8,128)(2,1)} %gather_fusion, pred[8192]{0:T(1024)(128)(4,1)S(1)} %get-tuple-element.5, pred[8192]{0:T(1024)(128)(4,1)S(1)} %get-tuple-element.7), kind=kLoop, calls=%fused_computation.6 | loop fusion | flops 33554432 | bytes 67125248 | tf_op jit(solution)/shard_map/jit(_where)/select_n | solution.py:27
  100.5 0.0 copy-start.3
  100.5 0.1 reduce-scatter.2.cloned.1.call-update
  100.6 0.1 all-gather.2.cloned.1.call-start
  100.7 0.6 copy-done.3
  101.2 170.6 %reduce-scatter.2.cloned.1.call-done = bf16[1,1024,2048]{2,1,0:T(8,128)(2,1)} async-done(((bf16[1,8192,2048]{2,1,0:T(8,128)(2,1)}), bf16[1,1024,2048]{2,1,0:T(8,128)(2,1)}) %reduce-scatter.2.cloned.1.call-update) | async-done | bytes 4194320 | tf_op jit(solution)/shard_map/reduce_scatter | solution.py:28
  271.8 0.0 copy-start
  271.8 0.0 copy-start.1
  271.8 3.2 fusion.12
  275.1 5.4 fusion.13
  280.5 0.0 copy-done
  280.5 0.0 copy-done.1
  280.5 0.0 copy-start.2
  280.6 3.7 fusion.10
  284.2 0.1 all-gather.2.cloned.1.call-update
  284.3 0.0 copy-done.2
  284.3 0.1 broadcast_select_fusion
  284.3 13.9 %psum.7 = f32[2048]{0:T(1024)} all-reduce(f32[2048]{0:T(1024)S(1)} %get-tuple-element.3), channel_id=1, replica_groups=mesh['dp'=4,'tp'=8] {'tp'}, use_global_device_ids=true, to_apply=%region_5.6 | all-reduce | flops 2048 | bytes 16384 | tf_op jit(solution)/shard_map/psum | solution.py:30
  298.3 5.2 fusion.14
  303.5 135.1 %all-gather.2.cloned.1.call-done = bf16[1,8192,2048]{2,1,0:T(8,128)(2,1)} async-done(((bf16[1,1024,2048]{2,1,0:T(8,128)(2,1)}), bf16[1,8192,2048]{2,1,0:T(8,128)(2,1)}) %all-gather.2.cloned.1.call-update) | async-done | bytes 33554448 | tf_op jit(solution)/shard_map/all_gather | solution.py:31
  438.6 119.0 %scatter_custom_fusion = f32[4000,2048]{1,0:T(8,128)} fusion(s32[8192]{0:T(1024)S(1)} %bitcast.13, bf16[1,8192,2048]{2,1,0:T(8,128)(2,1)} %all-gather.2.cloned.1.call-done, f32[]{:T(128)} %constant.15.clone.1), kind=kCustom, calls=%fused_computation.2 | custom fusion | flops 33554432 | bytes 66322436 | tf_op jit(solution)/shard_map/scatter-add | solution.py:33
  (4 shorter events, 0.0 us)
Async XLA Ops:
  7.2 264.7 %reduce-scatter.2.cloned.1.call-start = ((), (), s32[]{:S(2)}) async-start(), calls=%async_computation.1 | async-start | bytes 37748736 | tf_op jit(solution)/shard_map/reduce_scatter | solution.py:28
  100.5 0.7 copy-start.3
  100.6 338.0 %all-gather.2.cloned.1.call-start = ((), (), s32[]{:S(2)}) async-start(), calls=%async_computation.2 | async-start | bytes 37748736 | tf_op jit(solution)/shard_map/all_gather | solution.py:31
  271.8 8.7 %copy-start = (bf16[1,1024,2048]{2,1,0:T(8,128)(2,1)S(1)}, bf16[1,1024,2048]{2,1,0:T(8,128)(2,1)}, u32[]{:S(2)}) copy-start(bf16[1,1024,2048]{2,1,0:T(8,128)(2,1)} %reduce-scatter.2.cloned.1.call-done) | copy-start | bytes 12582916
  271.8 8.7 %copy-start.1 = (bf16[1,1024,2048]{2,1,0:T(8,128)(2,1)S(1)}, bf16[1,1024,2048]{2,1,0:T(8,128)(2,1)}, u32[]{:S(2)}) copy-start(bf16[1,1024,2048]{2,1,0:T(8,128)(2,1)} %param.7) | copy-start | bytes 12582916
  280.5 3.7 copy-start.2
Sparse Core Ops, SparseCore 0:
  100.7 171.0 reduce-scatter.1
  284.4 154.1 all-gather.1
where the time goes:
time: 565 us; the launch traced here: 564 us
  waiting for transfers between devices  306 us (54%)
  other arithmetic  161 us (28%)
  local copies, waits for them, and re-layouts  69.7 us (12%)
  between operations  14.1 us (2%)
  blocking collectives  13.9 us (2%)
    reduce_scatter x1, waiting for transfers between devices, device_step(): lax.psum_scatter(partial_rows, 'tp', scatter_dimension=1, tiled=True)  171 us
    all_gather x1, waiting for transfers between devices, device_step(): grad_all = lax.all_gather(grad_in, 'tp', axis=1, tiled=True)  135 us
    scatter-add x1, other arithmetic, device_step(): jax.ops.segment_sum(grad_all.astype(jnp.float32).reshape(-1, hidden_size)...  119 us
    gather x1, local copies, waits for them, and re-layouts, device_step(): looked_up = jnp.take(table_block, jnp.where(owned, local_ids, 0), axis=0)  69.1 us
    select_n x1, other arithmetic, device_step(): jnp.where(owned[:, :, None], looked_up, jnp.zeros((), jnp.bfloat16))  23.1 us
    psum x1, blocking collectives, device_step(): grad_gain = lax.psum(gain_part, 'tp')  13.9 us
  transfers between devices with their start and end apart: 2, of which 2 were waited for; matrix products, arithmetic and copies ran while one was open for 1% of the time, Pallas kernels for 0%

commit v1 on v0

v1 whole, which is shorter than its diff:
```python
import functools

import jax
import jax.numpy as jnp
from jax import lax
from jax.experimental import pallas as pl
from jax.experimental.pallas import tpu as pltpu
from jax.sharding import PartitionSpec as P

RMS_EPS = 1e-5
MESH = pl.DeviceIdType.MESH
LANES = 128
CORES = 2
CAP = 112
CODE = 256
NT = (((1,), (1,)), ((), ()))
TN = (((0,), (0,)), ((), ()))
F32, BF16 = jnp.float32, jnp.bfloat16


def onehot(mask):
    return jnp.where(mask, 1.0, 0.0).astype(BF16)


def lists_kernel(n, rows, ids_ref, uid_ref, code_ref, top_ref, rank_ref):
    m, width = ids_ref.shape
    hb = -(-rows // LANES)
    high = n * hb
    me = lax.axis_index('tp')
    chip = me // CORES

    def split(ids):
        owner = jnp.zeros_like(ids)
        for k in range(1, n):
            owner += (ids >= k * rows).astype(jnp.int32)
        local = ids - owner * rows
        return owner, owner * hb + (local >> 7), local & (LANES - 1)

    def hots(hi, lo):
        h = onehot(lax.broadcasted_iota(jnp.int32, (high, width), 0) == hi)
        l = onehot(lax.broadcasted_iota(jnp.int32, (LANES, width), 0) == lo)
        return h, l

    a = lax.broadcasted_iota(jnp.int32, (LANES, LANES), 0)
    b = lax.broadcasted_iota(jnp.int32, (LANES, LANES), 1)
    upper, ones = onehot(a <= b), jnp.ones((LANES, LANES), BF16)
    ra = lax.broadcasted_iota(jnp.int32, (high, high), 0)
    rb = lax.broadcasted_iota(jnp.int32, (high, high), 1)
    first = jnp.zeros_like(ra)
    for k in range(1, n):
        first += jnp.where(ra >= k * hb, hb, 0)
    before = onehot((rb < ra) & (rb >= first))

    top = jnp.full((high, LANES), -1.0, F32)
    for j in range(m):
        _, hi, lo = split(ids_ref[j:j + 1, :])
        h, l = hots(hi, lo)
        count = lax.dot_general(h, l, NT, preferred_element_type=F32)
        here = count > 0.5
        present = onehot(here)
        upto = jnp.dot(present, upper, preferred_element_type=F32)
        total = jnp.dot(present, ones, preferred_element_type=F32).astype(BF16)
        base = jnp.dot(before, total, preferred_element_type=F32)
        rank = jnp.where(here, base + upto - 1.0, -1.0)
        top = jnp.maximum(top, rank)
        rank_ref[j] = jnp.minimum(rank, CODE - 1.0)
    top_ref[...] = jnp.broadcast_to(jnp.max(top, axis=(0, 1), keepdims=True), top_ref.shape)

    owner, hi, lo = split(ids_ref[pl.ds(chip, 1), :])
    h, l = hots(hi, lo)
    picked = lax.dot_general(rank_ref[chip].astype(BF16), h, TN, preferred_element_type=F32)
    place = jnp.sum(picked * l.astype(F32), axis=0, keepdims=True)
    code_ref[...] = owner.astype(F32) * CODE + place

    want = lax.broadcasted_iota(jnp.int32, (CAP, LANES), 0).astype(F32)
    lane = lax.broadcasted_iota(jnp.int32, (1, LANES), 1)
    for j in range(m):
        mine = rank_ref[j, pl.ds(pl.multiple_of(me * hb, hb), hb), :]
        found = jnp.zeros((CAP, LANES), jnp.int32)
        for k in range(hb):
            found += jnp.where(mine[k:k + 1, :] == want, k * LANES + lane, 0)
        ids = jnp.sum(found.astype(F32), axis=1, keepdims=True).astype(jnp.int32)
        uid_ref[j * CAP:(j + 1) * CAP, :] = jnp.broadcast_to(ids, (CAP, LANES))


def make_lists(token_ids, n, rows):
    m = n // CORES
    ids = token_ids.reshape(m, -1)
    hb = -(-rows // LANES)
    vm = pl.BlockSpec(memory_space=pltpu.VMEM)
    return pl.pallas_call(
        functools.partial(lists_kernel, n, rows),
        out_shape=(
            jax.ShapeDtypeStruct((m * CAP, LANES), jnp.int32),
            jax.ShapeDtypeStruct((1, ids.shape[1]), F32),
            jax.ShapeDtypeStruct((8, LANES), F32),
        ),
        in_specs=[vm],
        out_specs=(vm, vm, vm),
        scratch_shapes=[pltpu.VMEM((m, n * hb, LANES), F32)],
        name='lists',
    )(ids)


def barrier(n, me):
    sem = pltpu.get_barrier_semaphore()
    for k in range(1, n):
        pl.semaphore_signal(sem, inc=1, device_id={'tp': lax.rem(me + k, n)}, device_id_type=MESH)
    pl.semaphore_wait(sem, n - 1)


def core_kernel(n, rows_ref, code_ref, tgt_ref, gain_ref, dy_hbm, y_hbm, sums_hbm, dg_ref,
                got, relay, dy, y, dx, xs, psend, prelay, dgacc, dgs,
                fsend, frecv, bsend, brecv, tsend, trecv, gsend, grecv, local):
    m = n // CORES
    tokens, hidden = dy_hbm.shape
    tile, sub = 128, 16
    tiles = tokens // tile
    me = lax.axis_index('tp')
    chip, core = me // CORES, lax.rem(me, CORES)
    step = 1 - 2 * core
    ahead, behind, far = (lax.rem(chip + step + m, m), lax.rem(chip - step + m, m), lax.rem(chip + 2, m))
    sib = chip * CORES + 1 - core

    def dev(c):
        return c * CORES + core

    def remote(src, dst, s, r, d):
        return pltpu.make_async_remote_copy(
            src_ref=src, dst_ref=dst, send_sem=s, recv_sem=r, device_id={'tp': d}, device_id_type=MESH)

    def slot(d):
        return got.at[pl.ds(pl.multiple_of(d * CAP, CAP), CAP)]

    dy_in = pltpu.make_async_copy(dy_hbm, dy, local.at[0])
    dy_in.start()
    own = pltpu.make_async_copy(rows_ref.at[chip], slot(me), local.at[1])
    own.start()
    barrier(n, me)

    to_far = remote(rows_ref.at[far], relay, fsend.at[0], frecv.at[n], dev(ahead))
    to_far.start()
    to_behind = remote(rows_ref.at[behind], slot(me), fsend.at[2], frecv.at[me], dev(behind))
    to_behind.start()
    to_ahead = remote(rows_ref.at[ahead], slot(me), fsend.at[1], frecv.at[me], dev(ahead))
    to_ahead.start()
    to_sib = remote(rows_ref.at[chip], slot(me), fsend.at[3], frecv.at[me], sib)
    to_sib.start()
    to_far.wait_recv()
    passed = remote(relay, slot(dev(behind)), fsend.at[4], frecv.at[dev(behind)], dev(ahead))
    passed.start()
    shared = []
    for k, source in enumerate((ahead, behind, far)):
        d = dev(source)
        share = remote(slot(d), slot(d), fsend.at[5 + k], frecv.at[d], sib)
        share.wait_recv()
        share.start()
        shared.append(share)
    for source in (chip, ahead, behind, far):
        d = source * CORES + 1 - core
        remote(slot(d), slot(d), fsend.at[3], frecv.at[d], sib).wait_recv()
    own.wait()
    dy_in.wait()

    dgacc[...] = jnp.zeros_like(dgacc)
    gain = gain_ref[...].astype(F32)

    def mine(t):
        return dx.at[pl.ds(pl.multiple_of(core * tokens + t * tile, tile), tile)]

    def swap(t):
        return remote(mine(t), mine(t), tsend.at[t], trecv.at[t], sib)

    def y_out(t):
        where = pl.ds(pl.multiple_of(t * tile, tile), tile)
        return pltpu.make_async_copy(y.at[where], y_hbm.at[where], local.at[2])

    def norm_tile(t, carry):
        at = pl.multiple_of(core * tokens + t * tile, tile)
        codes = jnp.broadcast_to(code_ref[:, pl.ds(at, tile)], (LANES, tile)).T
        pick = jnp.concatenate(
            [onehot(codes == tgt_ref[:, k:k + LANES]) for k in range(0, tgt_ref.shape[1], LANES)], axis=1)
        xs[...] = jnp.dot(pick, got[...], preferred_element_type=F32)

        def piece(k, c):
            here = pl.ds(pl.multiple_of(k * sub, sub), sub)
            glob = pl.ds(pl.multiple_of(t * tile + k * sub, sub), sub)
            h = xs[here, :]
            r = lax.rsqrt(jnp.mean(h * h, axis=-1, keepdims=True) + RMS_EPS)
            xh = h * r
            y[glob, :] = (xh.astype(BF16).astype(F32) * gain).astype(BF16)
            g = dy[glob, :].astype(F32)
            part = g * xh
            dgacc[...] += part[:8] + part[8:]
            u = g * gain
            mean = jnp.mean(u * xh, axis=-1, keepdims=True)
            dx[pl.ds(pl.multiple_of(at + k * sub, sub), sub), :] = (r * (u - xh * mean)).astype(BF16)
            return c

        lax.fori_loop(0, tile // sub, piece, 0)
        swap(t).start()
        return carry

    lax.fori_loop(0, tiles, norm_tile, 0)
    y_copy = pltpu.make_async_copy(y, y_hbm, local.at[2])
    y_copy.start()

    dgs[me] = jnp.sum(dgacc[...], axis=0, keepdims=True)
    for k in range(1, n):
        remote(dgs.at[me], dgs.at[me], gsend.at[k], grecv.at[k], lax.rem(me + k, n)).start()

    def swapped(t, carry):
        swap(t).wait()
        return carry

    lax.fori_loop(0, tiles, swapped, 0)

    wide = 512
    place = lax.broadcasted_iota(jnp.int32, (CAP, CORES * tokens), 0)

    def sums(q, dest):
        pick = onehot((place + dev(dest) * CODE).astype(F32) == code_ref[...])

        def part(k, c):
            cols = pl.ds(pl.multiple_of(k * wide, wide), wide)
            psend[q, :, cols] = jnp.dot(pick, dx[:, cols], preferred_element_type=F32)
            return c

        lax.fori_loop(0, hidden // wide, part, 0)

    sums(0, far)
    back_far = remote(psend.at[0], prelay, bsend.at[0], brecv.at[m], dev(ahead))
    back_far.start()
    sums(1, behind)
    back_behind = remote(psend.at[1], sums_hbm.at[chip], bsend.at[1], brecv.at[chip], dev(behind))
    back_behind.start()
    sums(2, ahead)
    back_ahead = remote(psend.at[2], sums_hbm.at[chip], bsend.at[2], brecv.at[chip], dev(ahead))
    back_ahead.start()
    sums(3, chip)
    keep = pltpu.make_async_copy(psend.at[3], sums_hbm.at[chip], local.at[3])
    keep.start()
    back_far.wait_recv()
    back_pass = remote(prelay, sums_hbm.at[behind], bsend.at[3], brecv.at[behind], dev(ahead))
    back_pass.start()

    for k in range(1, n):
        remote(dgs.at[me], dgs.at[lax.rem(me - k + n, n)], gsend.at[k], grecv.at[k], sib).wait()
    total = dgs[0]
    for k in range(1, n):
        total = total + dgs[k]
    dg_ref[...] = total

    for k, source in enumerate((ahead, behind, far)):
        remote(psend.at[0], sums_hbm.at[source], bsend.at[0], brecv.at[source], sib).wait_recv()
    for copy in (to_far, to_behind, to_ahead, to_sib, passed, *shared, back_far, back_behind, back_ahead, back_pass):
        copy.wait_send()
    keep.wait()
    y_copy.wait()


def short_path(n, table, uid, code, gain, grad):
    m = n // CORES
    _, tokens, hidden = grad.shape
    take = uid[:, 0]
    send = jnp.take(table, take, axis=0, mode='clip').reshape(m, CAP, hidden)
    k = jnp.arange(n * CAP)
    tgt = ((k // CAP) * CODE + k % CAP).astype(F32)[None]
    vm = pl.BlockSpec(memory_space=pltpu.VMEM)
    hbm = pl.BlockSpec(memory_space=pl.ANY)
    dma = pltpu.SemaphoreType.DMA
    tiles = tokens // 128
    y, sums, dg = pl.pallas_call(
        functools.partial(core_kernel, n),
        out_shape=(
            jax.ShapeDtypeStruct((tokens, hidden), BF16),
            jax.ShapeDtypeStruct((m, CAP, hidden), F32),
            jax.ShapeDtypeStruct((1, hidden), F32),
        ),
        in_specs=[vm, vm, vm, vm, hbm],
        out_specs=(hbm, hbm, vm),
        scratch_shapes=[
            pltpu.VMEM((n * CAP, hidden), BF16),
            pltpu.VMEM((CAP, hidden), BF16),
            pltpu.VMEM((tokens, hidden), BF16),
            pltpu.VMEM((tokens, hidden), BF16),
            pltpu.VMEM((CORES * tokens, hidden), BF16),
            pltpu.VMEM((128, hidden), F32),
            pltpu.VMEM((m, CAP, hidden), F32),
            pltpu.VMEM((CAP, hidden), F32),
            pltpu.VMEM((8, hidden), F32),
            pltpu.VMEM((n, 1, hidden), F32),
            dma((8,)), dma((n + 1,)), dma((m,)), dma((m + 1,)), dma((tiles,)), dma((tiles,)), dma((n,)), dma((n,)),
            dma((4,)),
        ],
        compiler_params=pltpu.CompilerParams(
            collective_id=0, has_side_effects=True, vmem_limit_bytes=60 * 1024 * 1024),
        name='short_path',
    )(send, code, tgt, gain.reshape(1, hidden), grad[0])
    table_grad = jnp.zeros((table.shape[0], hidden), F32).at[take].add(sums.reshape(m * CAP, hidden), mode='drop')
    return y[None], table_grad, dg[0]


def exchange_kernel(n, per_dest, src, out, send, recv, local):
    me = lax.axis_index('tp')

    def block(d):
        return src.at[d] if per_dest else src

    barrier(n, me)
    own = pltpu.make_async_copy(block(me), out.at[me], local)
    own.start()
    copies = []
    for k in range(1, n):
        peer = lax.rem(me + k, n)
        copies.append(pltpu.make_async_remote_copy(
            src_ref=block(peer), dst_ref=out.at[me], send_sem=send.at[k], recv_sem=recv.at[k],
            device_id={'tp': peer}, device_id_type=MESH))
        copies[-1].start()
    own.wait()
    for copy in copies:
        copy.wait()


def exchange(n, src, collective_id, per_dest):
    shape = src.shape[1:] if per_dest else src.shape
    hbm = pl.BlockSpec(memory_space=pl.ANY)
    dma = pltpu.SemaphoreType.DMA
    return pl.pallas_call(
        functools.partial(exchange_kernel, n, per_dest),
        out_shape=jax.ShapeDtypeStruct((n, *shape), src.dtype),
        in_specs=[hbm],
        out_specs=hbm,
        scratch_shapes=[dma((n,)), dma((n,)), dma(())],
        compiler_params=pltpu.CompilerParams(collective_id=collective_id, has_side_effects=True),
        name=f'exchange{collective_id}',
    )(src)


def norm_pass(embedded, norm_gain, grad_block):
    hidden_f32 = embedded.astype(F32)
    inv_rms = lax.rsqrt(jnp.mean(hidden_f32 * hidden_f32, axis=-1, keepdims=True) + RMS_EPS)
    x_hat = hidden_f32 * inv_rms
    normed = x_hat.astype(BF16) * norm_gain
    grad_f32 = grad_block.astype(F32)
    gain_part = jnp.sum(grad_f32 * x_hat, axis=(0, 1))
    grad_hat = grad_f32 * norm_gain.astype(F32)
    grad_in = (inv_rms * (grad_hat - x_hat * jnp.mean(grad_hat * x_hat, axis=-1, keepdims=True))).astype(BF16)
    return normed, grad_in, gain_part


def dense_path(n, token_ids, table, gain, grad):
    rows, hidden = table.shape
    tokens = grad.shape[1]
    local_ids = token_ids.reshape(-1) - lax.axis_index('tp') * rows
    owned = (local_ids >= 0) & (local_ids < rows)
    looked_up = jnp.take(table, jnp.where(owned, local_ids, 0), axis=0)
    partial = jnp.where(owned[:, None], looked_up, jnp.zeros((), BF16)).reshape(n, tokens, hidden)
    embedded = jnp.sum(exchange(n, partial, 1, True).astype(F32), axis=0).astype(BF16)
    normed, grad_in, gain_part = norm_pass(embedded[None], gain, grad)
    grad_gain = jnp.sum(exchange(n, gain_part.reshape(-1, LANES), 2, False), axis=0).reshape(-1)
    grad_all = exchange(n, grad_in[0], 3, False).reshape(-1, hidden)
    segments = jnp.where(owned, local_ids, rows)
    table_grad = jax.ops.segment_sum(grad_all.astype(F32), segments, num_segments=rows)
    return normed, table_grad, grad_gain


def device_step(n, token_ids, table, gain, grad):
    uid, code, top = make_lists(token_ids, n, table.shape[0])
    fits = top[0, 0] < CAP
    return lax.cond(
        fits,
        lambda: short_path(n, table, uid, code, gain, grad),
        lambda: dense_path(n, token_ids, table, gain, grad),
    )


def solution(mesh):
    n = mesh.shape['tp']
    return jax.shard_map(
        functools.partial(device_step, n), mesh=mesh,
        in_specs=(P('dp', None), P('tp', None), P(None), P('dp', 'tp', None)),
        out_specs=(P('dp', 'tp', None), P(('dp', 'tp'), None), P('dp')), check_vma=False)
```

time: 565 us -> 148 us (0.26)
  waiting for transfers between devices: 306 us -> 0 us
  other arithmetic: 161 us -> 23.4 us
  Pallas kernels: 0 us -> 101 us
  local copies, waits for them, and re-layouts: 69.7 us -> 22 us
  blocking collectives: 13.9 us -> 0 us
  between operations: 14.1 us -> 1.29 us
    reduce_scatter x1 -> x0, waiting for transfers between devices: 171 us -> none  [device_step(): lax.psum_scatter(partial_rows, 'tp', scatter_dimension=1, tiled=True)]
    all_gather x1 -> x0, waiting for transfers between devices: 135 us -> none  [device_step(): grad_all = lax.all_gather(grad_in, 'tp', axis=1, tiled=True)]
    pallas_call x0 -> x2, Pallas kernels: none -> 101 us  [the longest x1 95 us: short_path(): pl.pallas_call(functools.partial(core_kernel, n), out_shape=(jax.ShapeDty...]
    scatter-add x1, other arithmetic: 119 us -> 21.3 us  [short_path(): jnp.zeros((table.shape[0], hidden), F32).at[take]]
    gather x1, local copies, waits for them, and re-layouts: 69.1 us -> 12.9 us  [short_path(): send = jnp.take(table, take, axis=0, mode='clip').reshape(m, CAP, hidden)]
    select_n x2 -> x1, other arithmetic: 23.2 us -> 0.01 us  [short_path(): jnp.zeros((table.shape[0], hidden), F32).at[take]]
    psum x1 -> x0, blocking collectives: 13.9 us -> none  [device_step(): grad_gain = lax.psum(gain_part, 'tp')]
    reduce_sum x2 -> x0, other arithmetic: 8.67 us -> none  [the longest x1 5.45 us: norm_pass(): gain_part = jnp.sum(grad_f32 * x_hat, axis=(0, 1))]
  transfers between devices with their start and end apart: 2 -> 0, of which waited for: 2 -> 0; matrix products, arithmetic and copies ran while one was open for 1% -> 0% of each run, Pallas kernels for 0% -> 0%
where the time goes in v1:
time: 148 us
  Pallas kernels  101 us (68%)
  other arithmetic  23.4 us (16%)
  local copies, waits for them, and re-layouts  22 us (15%)
    pallas_call x1, Pallas kernels, short_path(): pl.pallas_call(functools.partial(core_kernel, n), out_shape=(jax.ShapeDty...  95 us
    scatter-add x1, other arithmetic, short_path(): jnp.zeros((table.shape[0], hidden), F32).at[take]  21.3 us
    gather x1, local copies, waits for them, and re-layouts, short_path(): send = jnp.take(table, take, axis=0, mode='clip').reshape(m, CAP, hidden)  12.9 us
    unnamed x3, local copies, waits for them, and re-layouts  5.9 us
    pallas_call x1, Pallas kernels, make_lists(): pl.pallas_call(functools.partial(lists_kernel, n, rows), out_shape=(jax.S...  5.77 us

profile of v1, /device:TPU:81, one launch (start us, length us, event | category | flops | bytes accessed | tf_op | source)
XLA Modules:
  0.0 147.7 jit_solution(15182736244779936357)
XLA Ops:
  0.6 0.5 broadcast.338
  1.1 1.5 %reduce.10 = s32[8192]{0:T(1024)S(1)} reduce(s32[1,8192]{1,0:T(1,128)} %param.6, s32[]{:T(128)} %broadcast.338), dimensions={0}, to_apply=%param.6.reduce_sub_computation.3 | reduce | bytes 65540 | tf_op args[0]
  2.6 0.6 reshape.311.ids_ref
  3.3 5.8 %lists.1 = (s32[448,128]{1,0:T(8,128)S(1)}, f32[1,2048]{1,0:T(1,128)S(1)}, f32[8,128]{1,0:T(8,128)}) custom-call(s32[4,2048]{1,0:T(4,128)} %reshape.311.ids_ref), custom_call_target="tpu_custom_call" | custom-call | tf_op jit(solution)/shard_map/lists/pallas_call | solution.py:91
  9.0 1.2 slice.6
  10.9 131.4 %conditional.1 = (bf16[1,1024,2048]{2,1,0:T(8,128)(2,1)}, f32[4000,2048]{1,0:T(8,128)}, f32[2048]{0:T(1024)S(1)}) conditional(s32[]{:T(128)} %bitcast.17, (s32[1,8192]{1,0:T(1,128)}, bf16[4000,2048]{1,0:T(8,128)(2,1)}, bf16[2048]{0:T(1024)(128)(2,1)}, bf16[1,1024,2048]{2,1,0:T(8,128)(2,1)}) %tuple.15, (s32[448,128]{1,0:T(8,128)S(1)}, ...), branch_computations={%region_0.7_spmd, %region_7.9_spmd} | conditional | flops 130210816 | bytes 289186432 | solution.py:371
  11.1 0.6 fusion.3.tgt_ref
  11.7 1.3 reshape.308.gain_ref
  13.0 0.1 copy.13
  13.2 12.9 %gather_fusion = bf16[448,2048]{1,0:T(8,128)(2,1)} fusion(bf16[4000,2048]{1,0:T(8,128)(2,1)} %get-tuple-element.22, s32[1024]{0:T(1024)S(1)} %pad_clamp_fusion), kind=kCustom, calls=%fused_computation.1 | custom fusion | bytes 3671808 | tf_op jit(solution)/shard_map/cond/branch_1_fun/jit(_take)/gather | solution.py:266
  26.1 95.0 %short_path.1 = (bf16[1024,2048]{1,0:T(8,128)(2,1)}, f32[4,112,2048]{2,1,0:T(8,128)}, f32[1,2048]{1,0:T(1,128)S(1)}) custom-call(bf16[4,112,2048]{2,1,0:T(8,128)(2,1)} %bitcast.42, f32[1,2048]{1,0:T(1,128)S(1)} %get-tuple-element.24.code_ref, f32[1,896]{1,0:T(1,128)} %fusion.3.tgt_ref, bf16[1,2048]{1,0:T(2,128)(2,1)} %reshape.308.gain_ref, ...), custom_call_target="tpu_custom_call" | custom-call | tf_op jit(solution)/shard_map/cond/branch_1_fun/short_path/pallas_call | solution.py:273
  121.1 21.3 %scatter_custom_fusion.1 = f32[4000,2048]{1,0:T(8,128)} fusion(s32[448]{0:T(512)S(1)} %bitcast.49, f32[448,2048]{1,0:T(8,128)} %bitcast.50, f32[]{:T(128)} %constant.63.clone), kind=kCustom, calls=%fused_computation.4 | custom fusion | flops 917504 | bytes 32768512 | tf_op jit(solution)/shard_map/cond/branch_1_fun/scatter-add | solution.py:300
  142.3 4.8 %copy.22 = bf16[1,1024,2048]{2,1,0:T(8,128)(2,1)} copy(bf16[1,1024,2048]{2,1,0:T(8,128)(2,1)} %get-tuple-element.64) | data formatting | bytes 8388608
  147.1 0.6 copy.23
  (2 shorter events, 0.0 us)

commit v2 on v1

v2 whole, which is shorter than its diff:
```python
import functools

import jax
import jax.numpy as jnp
from jax import lax
from jax.experimental import pallas as pl
from jax.experimental.pallas import tpu as pltpu
from jax.sharding import PartitionSpec as P

RMS_EPS = 1e-5
MESH = pl.DeviceIdType.MESH
LANES = 128
CORES = 2
CAP = 112
MULTI = 56
SINGLE = 72
UNION = 240
CODE = 256
STRIDE = 128
PARTS = 4
TILE = 128
BF16_MAX = 3.3895313892515355e38
NT = (((1,), (1,)), ((), ()))
TN = (((0,), (0,)), ((), ()))
F32, BF16 = jnp.float32, jnp.bfloat16


def onehot(mask):
    return jnp.where(mask, 1.0, 0.0).astype(BF16)


def lists_kernel(n, rows, ids_ref, table_hbm, uid_ref, kmap_ref, code_ref, send_ref, fits_ref,
                 table, picked, rank_f, rank_b, rank_u, uid_s, sem):
    m = n // CORES
    width = ids_ref.shape[1] // m
    hb = -(-rows // LANES)
    high = n * hb
    me = lax.axis_index('tp')
    chip = me // CORES
    table_in = pltpu.make_async_copy(table_hbm, table, sem.at[0])
    table_in.start()
    picked[...] = jnp.zeros_like(picked)

    def split(ids):
        owner = jnp.zeros_like(ids)
        for k in range(1, n):
            owner += (ids >= k * rows).astype(jnp.int32)
        local = ids - owner * rows
        return owner, owner * hb + (local >> 7), local & (LANES - 1)

    def hots(hi, lo):
        h = onehot(lax.broadcasted_iota(jnp.int32, (high, width), 0) == hi)
        l = onehot(lax.broadcasted_iota(jnp.int32, (LANES, width), 0) == lo)
        return h, l

    a = lax.broadcasted_iota(jnp.int32, (LANES, LANES), 0)
    b = lax.broadcasted_iota(jnp.int32, (LANES, LANES), 1)
    lower, ones = onehot(a < b), jnp.ones((LANES, LANES), BF16)
    ra = lax.broadcasted_iota(jnp.int32, (high, high), 0)
    rb = lax.broadcasted_iota(jnp.int32, (high, high), 1)
    first = jnp.zeros_like(ra)
    for k in range(1, n):
        first += jnp.where(ra >= k * hb, hb, 0)
    before = onehot((rb < ra) & (rb >= first))

    def ahead_of(mask):
        present = onehot(mask)
        inside = jnp.dot(present, lower, preferred_element_type=F32)
        total = jnp.dot(present, ones, preferred_element_type=F32).astype(BF16)
        return inside + jnp.dot(before, total, preferred_element_type=F32)

    def over(mask, rank, cap):
        return jnp.where(mask & (rank > cap - 0.5), 1.0, 0.0)

    union = jnp.zeros((high, LANES), F32)
    bad = jnp.zeros((high, LANES), F32)
    for j in range(m):
        _, hi, lo = split(ids_ref[:, j * width:(j + 1) * width])
        h, l = hots(hi, lo)
        count = lax.dot_general(h, l, NT, preferred_element_type=F32)
        union += count
        here, many = count > 0.5, count > 1.5
        all_before, many_before = ahead_of(here), ahead_of(many)
        one_before = all_before - many_before
        bad += over(here, all_before, CAP) + over(many, many_before, MULTI) + over(count == 1.0, one_before, SINGLE)
        back = jnp.where(many, many_before, one_before + MULTI)
        rank_f[j] = jnp.where(here, jnp.minimum(all_before, CODE - 1.0), -1.0)
        rank_b[j] = jnp.where(here, jnp.minimum(back, CODE - 1.0), -1.0)
    here = union > 0.5
    all_before = ahead_of(here)
    bad += over(here, all_before, UNION)
    rank_u[...] = jnp.where(here, jnp.minimum(all_before, CODE - 1.0), -1.0)
    fits_ref[0, 0] = (jnp.max(bad) < 0.5).astype(jnp.int32)

    block = pl.ds(pl.multiple_of(me * hb, hb), hb)
    of_union = rank_u[block, :]
    lane = lax.broadcasted_iota(jnp.int32, (1, LANES), 1)
    every = jnp.ones((8, LANES), F32)

    def places(height):
        return lax.broadcasted_iota(jnp.int32, (height, LANES), 0).astype(F32)

    def as_row(found):
        return lax.dot_general(every, found, NT, preferred_element_type=F32, precision=lax.Precision.HIGHEST)[:1, :]

    want = places(CODE)
    found = jnp.zeros((CODE, LANES), F32)
    for k in range(hb):
        found += jnp.where(of_union[k:k + 1, :] == want, (k * LANES + lane).astype(F32), 0.0)
    length = jnp.max(of_union) + 1.0
    place = lax.broadcasted_iota(jnp.int32, (1, CODE), 1).astype(F32)
    uid_ref[...] = jnp.full(uid_ref.shape, rows, jnp.int32)
    uid_ref[:1, :] = jnp.where((place < length) & (place < UNION), as_row(found), float(rows)).astype(jnp.int32)
    uid_in = pltpu.make_async_copy(uid_ref, uid_s, sem.at[1])
    uid_in.start()

    owner, hi, lo = split(ids_ref[:, pl.ds(pl.multiple_of(chip * width, width), width)])
    h, l = hots(hi, lo)
    l = l.astype(F32)
    for k, rank in enumerate((rank_f, rank_b)):
        found = lax.dot_general(rank[chip].astype(BF16), h, TN, preferred_element_type=F32)
        code_ref[k:k + 1, :] = owner.astype(F32) * CODE + jnp.sum(found * l, axis=0, keepdims=True)

    want = places(LANES)
    spread = []
    for j in range(m):
        fwd, back = rank_f[j, block, :], rank_b[j, block, :]
        found_f = jnp.zeros((CAP, LANES), F32)
        found_b = jnp.zeros((LANES, LANES), F32)
        for k in range(hb):
            u = of_union[k:k + 1, :]
            found_f += jnp.where(fwd[k:k + 1, :] == want[:CAP], u, 0.0)
            found_b += jnp.where(back[k:k + 1, :] == want, u + 1.0, 0.0)
        of_slot = jnp.sum(found_f, axis=1, keepdims=True)
        spread.append(onehot(lax.broadcasted_iota(jnp.int32, (CAP, CODE), 1).astype(F32) == of_slot))
        row = as_row(found_b) - 1.0
        again = jnp.where(lane < MULTI, row, jnp.where(lane < 2 * MULTI, pltpu.roll(row, MULTI, 1), -1.0))
        kmap_ref[j:j + 1, :] = jnp.concatenate([row, again], axis=1)

    uid_in.wait()
    table_in.wait()
    pack, eight = 16, 8
    sublane = lax.broadcasted_iota(jnp.int32, (eight, table.shape[2]), 0)
    groups = jnp.minimum((length.astype(jnp.int32) + pack - 1) // pack, UNION // pack)

    def pick(q, carry):
        halves = []
        for half in range(pack // eight):
            acc = jnp.zeros(sublane.shape, F32)
            for k in range(eight):
                v = jnp.minimum(uid_s[0, q * pack + half * eight + k], rows - 1)
                tile = table[v // eight].astype(F32)
                turned = pltpu.roll(tile, lax.rem(k + eight - lax.rem(v, eight), eight), 0)
                acc = jnp.where(sublane == k, turned, acc)
            halves.append(acc)
        picked[pl.ds(pl.multiple_of(q * pack, pack), pack), :] = jnp.concatenate(halves, axis=0).astype(BF16)
        return carry

    lax.fori_loop(0, groups, pick, 0)
    for j in range(m):
        send_ref[j] = jnp.dot(spread[j], picked[...], preferred_element_type=F32).astype(BF16)


def make_lists(token_ids, table, n):
    m = n // CORES
    rows, hidden = table.shape
    hb = -(-rows // LANES)
    vm = pl.BlockSpec(memory_space=pltpu.VMEM)
    return pl.pallas_call(
        functools.partial(lists_kernel, n, rows),
        out_shape=(
            jax.ShapeDtypeStruct((8, CODE), jnp.int32),
            jax.ShapeDtypeStruct((m, 2 * LANES), F32),
            jax.ShapeDtypeStruct((2, token_ids.shape[1] // m), F32),
            jax.ShapeDtypeStruct((m, CAP, hidden), BF16),
            jax.ShapeDtypeStruct((1, 1), jnp.int32),
        ),
        in_specs=[vm, pl.BlockSpec(memory_space=pl.ANY)],
        out_specs=(vm, vm, vm, vm, pl.BlockSpec(memory_space=pltpu.SMEM)),
        scratch_shapes=[
            pltpu.VMEM((rows // 8, 8, hidden), BF16),
            pltpu.VMEM((CODE, hidden), BF16),
            pltpu.VMEM((m, n * hb, LANES), F32),
            pltpu.VMEM((m, n * hb, LANES), F32),
            pltpu.VMEM((n * hb, LANES), F32),
            pltpu.SMEM((8, CODE), jnp.int32),
            pltpu.SemaphoreType.DMA((2,)),
        ],
        compiler_params=pltpu.CompilerParams(vmem_limit_bytes=44 * 1024 * 1024),
        name='lists',
    )(token_ids, table.reshape(rows // 8, 8, hidden))


def barrier(n, me):
    sem = pltpu.get_barrier_semaphore()
    for k in range(1, n):
        pl.semaphore_signal(sem, inc=1, device_id={'tp': lax.rem(me + k, n)}, device_id_type=MESH)
    pl.semaphore_wait(sem, n - 1)


def core_kernel(n, rows_ref, code_ref, kmap_ref, gain_ref, dy_hbm, y, merged, dg_ref,
                got, relay, dy, dx, xs, codes, pick_x, psum, pone, rsum, rone, gsum, gone, dgacc, dgs,
                fsend, frecv, bsend, brecv, psend, precv, tsend, trecv, gsend, grecv, local):
    m = n // CORES
    tokens, hidden = dy_hbm.shape
    tiles = tokens // TILE
    me = lax.axis_index('tp')
    chip, core = me // CORES, lax.rem(me, CORES)
    step = 1 - 2 * core
    ahead, behind, far = (lax.rem(chip + step + m, m), lax.rem(chip - step + m, m), lax.rem(chip + 2, m))
    sib = chip * CORES + 1 - core

    def dev(c):
        return c * CORES + core

    def remote(src, dst, s, r, d):
        return pltpu.make_async_remote_copy(
            src_ref=src, dst_ref=dst, send_sem=s, recv_sem=r, device_id={'tp': d}, device_id_type=MESH)

    def slot(d):
        return got.at[pl.ds(pl.multiple_of(d * STRIDE, STRIDE), CAP)]

    dy_in = pltpu.make_async_copy(dy_hbm, dy, local.at[0])
    dy_in.start()
    own = pltpu.make_async_copy(rows_ref.at[chip], slot(me), local.at[1])
    own.start()
    barrier(n, me)

    to_far = remote(rows_ref.at[far], relay, fsend.at[0], frecv.at[n], dev(ahead))
    to_far.start()
    to_behind = remote(rows_ref.at[behind], slot(me), fsend.at[2], frecv.at[me], dev(behind))
    to_behind.start()
    to_ahead = remote(rows_ref.at[ahead], slot(me), fsend.at[1], frecv.at[me], dev(ahead))
    to_ahead.start()
    to_sib = remote(rows_ref.at[chip], slot(me), fsend.at[3], frecv.at[me], sib)
    to_sib.start()

    lane = lax.broadcasted_iota(jnp.int32, (1, LANES), 1).astype(F32)
    for d in range(n):
        got[d * STRIDE + CAP:(d + 1) * STRIDE, :] = jnp.zeros((STRIDE - CAP, hidden), BF16)
    dgacc[...] = jnp.zeros_like(dgacc)

    def turn(t, carry):
        at = pl.multiple_of(core * tokens + t * TILE, TILE)
        codes[pl.ds(pl.multiple_of(t * TILE, TILE), TILE), :] = jnp.broadcast_to(
            code_ref[:1, pl.ds(at, TILE)], (LANES, TILE)).T
        return carry

    lax.fori_loop(0, tiles, turn, 0)
    wide = hidden // PARTS

    def add_rows(source, init):
        for o in range(CORES):
            base = ((source * CORES + o) * CODE).astype(F32)
            pick_x[:, o * LANES:(o + 1) * LANES] = onehot(codes[...] == lane + base)
        rows = pl.ds(pl.multiple_of(source * CORES * STRIDE, CORES * STRIDE), CORES * STRIDE)

        def part(k, c):
            cols = pl.ds(pl.multiple_of(k * wide, wide), wide)
            term = jnp.dot(pick_x[...], got[rows, cols], preferred_element_type=F32)
            if init:
                xs[:, cols] = term
            else:
                xs[:, cols] += term
            return c

        lax.fori_loop(0, hidden // wide, part, 0)

    def from_sib(source):
        d = source * CORES + 1 - core
        remote(slot(d), slot(d), fsend.at[3], frecv.at[d], sib).wait_recv()

    shared = []

    def share(k, source):
        d = dev(source)
        copy = remote(slot(d), slot(d), fsend.at[5 + k], frecv.at[d], sib)
        copy.wait_recv()
        copy.start()
        shared.append(copy)

    own.wait()
    from_sib(chip)
    add_rows(chip, True)
    to_far.wait_recv()
    passed = remote(relay, slot(dev(behind)), fsend.at[4], frecv.at[dev(behind)], dev(ahead))
    passed.start()
    share(0, ahead)
    share(1, behind)
    for source in (behind, ahead):
        from_sib(source)
        add_rows(source, False)
    share(2, far)
    from_sib(far)
    add_rows(far, False)
    dy_in.wait()

    gain = gain_ref[...].astype(F32).reshape(1, hidden)
    columns = range(0, hidden, LANES)

    def mine(t):
        return dx.at[pl.ds(pl.multiple_of(core * tokens + t * TILE, TILE), TILE)]

    def swap(t):
        return remote(mine(t), mine(t), tsend.at[t], trecv.at[t], sib)

    def norm_tile(t, carry):
        here = pl.ds(pl.multiple_of(t * TILE, TILE), TILE)
        there = pl.ds(pl.multiple_of(core * tokens + t * TILE, TILE), TILE)
        acc = jnp.zeros((TILE, LANES), F32)
        for c in columns:
            h = xs[here, c:c + LANES]
            acc += h * h
        r = lax.rsqrt(jnp.sum(acc, axis=-1, keepdims=True) / hidden + RMS_EPS)
        r = jnp.broadcast_to(r, (TILE, LANES))
        acc = jnp.zeros((TILE, LANES), F32)
        for c in columns:
            xh = xs[here, c:c + LANES] * r
            gain_c = gain[:, c:c + LANES]
            y[here, c:c + LANES] = (xh.astype(BF16).astype(F32) * gain_c).astype(BF16)
            g = dy[here, c:c + LANES].astype(F32)
            part = g * xh
            acc += g * gain_c * xh
            dgacc[:, c:c + LANES] += jnp.sum(part.reshape(TILE // 8, 8, LANES), axis=0)
        mean = jnp.broadcast_to(jnp.sum(acc, axis=-1, keepdims=True) / hidden, (TILE, LANES))
        for c in columns:
            xh = xs[here, c:c + LANES] * r
            u = dy[here, c:c + LANES].astype(F32) * gain[:, c:c + LANES]
            dx[there, c:c + LANES] = (r * (u - xh * mean)).astype(BF16)
        swap(t).start()
        return carry

    lax.fori_loop(0, tiles, norm_tile, 0)

    dgs[me] = jnp.sum(dgacc[...], axis=0, keepdims=True)
    for k in range(1, n):
        remote(dgs.at[me], dgs.at[me], gsend.at[k], grecv.at[k], lax.rem(me + k, n)).start()

    def swapped(t, carry):
        swap(t).wait()
        return carry

    lax.fori_loop(0, tiles, swapped, 0)

    place = lax.broadcasted_iota(jnp.int32, (LANES, CORES * tokens), 0)

    def picks(dest):
        return onehot((place + dev(dest) * CODE).astype(F32) == code_ref[1:2, :])

    def sums(q, pick, k):
        cols = pl.ds(pl.multiple_of(k * wide, wide), wide)
        total = jnp.dot(pick, dx[:, cols], preferred_element_type=F32)
        psum[q, k] = total[:MULTI]
        pone[q, k] = total[MULTI:].astype(BF16)

    def all_sums(q, dest):
        pick = picks(dest)

        def part(k, c):
            sums(q, pick, k)
            return c

        lax.fori_loop(0, PARTS, part, 0)

    first, relays = [], []
    pick = picks(far)
    for k in range(PARTS):
        sums(0, pick, k)
        for w, (mine_, relay_) in enumerate(((psum, rsum), (pone, rone))):
            first.append(remote(mine_.at[0, k], relay_.at[k], psend.at[w, 0, k], precv.at[w, 0, k], dev(ahead)))
            first[-1].start()

    def back(q, dest, sem):
        out = []
        for w, (mine_, theirs) in enumerate(((psum, gsum), (pone, gone))):
            out.append(remote(mine_.at[q], theirs.at[chip], bsend.at[w, sem], brecv.at[w, chip], dev(dest)))
            out[-1].start()
        return out

    all_sums(1, behind)
    direct = back(1, behind, 0)
    all_sums(2, ahead)
    direct += back(2, ahead, 1)
    all_sums(3, chip)

    def merge(source, multi, single, init):
        index = kmap_ref[pl.ds(source, 1), :]
        pick = onehot(lax.broadcasted_iota(jnp.int32, (UNION, 2 * LANES), 0).astype(F32) == index)
        pad = jnp.zeros((2 * LANES - 3 * MULTI - SINGLE, wide), F32)

        def part(k, c):
            cols = pl.ds(pl.multiple_of(k * wide, wide), wide)
            p = multi[k]
            high = jnp.clip(p, -BF16_MAX, BF16_MAX).astype(BF16).astype(F32)
            rest = p - high
            mid = rest.astype(BF16).astype(F32)
            stack = jnp.concatenate([high, single[k].astype(F32), mid, rest - mid, pad], axis=0).astype(BF16)
            term = jnp.dot(pick, stack, preferred_element_type=F32)
            if init:
                merged[:, cols] = term
            else:
                merged[:, cols] += term
            return c

        lax.fori_loop(0, PARTS, part, 0)

    for k in range(PARTS):
        for w, (relay_, theirs) in enumerate(((rsum, gsum), (rone, gone))):
            first[2 * k + w].wait_recv()
            relays.append(remote(relay_.at[k], theirs.at[behind, k], psend.at[w, 1, k], precv.at[w, 1, k], dev(ahead)))
            relays[-1].start()
    merge(chip, psum.at[3], pone.at[3], True)

    for k in range(1, n):
        remote(dgs.at[me], dgs.at[lax.rem(me - k + n, n)], gsend.at[k], grecv.at[k], sib).wait()
    total = dgs[0]
    for k in range(1, n):
        total = total + dgs[k]
    dg_ref[...] = total

    for source in (ahead, behind):
        for w, (mine_, theirs) in enumerate(((psum, gsum), (pone, gone))):
            remote(mine_.at[0], theirs.at[source], bsend.at[w, 0], brecv.at[w, source], sib).wait_recv()
        merge(source, gsum.at[source], gone.at[source], False)
    for copy in relays:
        copy.wait_recv()
    merge(far, gsum.at[far], gone.at[far], False)
    for copy in (to_far, to_behind, to_ahead, to_sib, passed, *shared, *first, *direct, *relays):
        copy.wait_send()


def write_kernel(uid_s, merged_ref, y_ref, dg_ref, table_grad_ref, y_out, dg_out, at, sem):
    step, tile = pl.program_id(0), table_grad_ref.shape[0]
    y_copy = pltpu.make_async_copy(y_ref, y_out, sem.at[0])

    @pl.when(step == 0)
    def _():
        y_copy.start()
        dg_out[...] = dg_ref[...]
        at[0] = 0

    table_grad_ref[...] = jnp.zeros_like(table_grad_ref)

    def more(p):
        return uid_s[0, p] < (step + 1) * tile

    def put(p):
        table_grad_ref[pl.ds(uid_s[0, p] - step * tile, 1), :] = merged_ref[pl.ds(p, 1), :]
        return p + 1

    at[0] = lax.while_loop(more, put, at[0])

    @pl.when(step == pl.num_programs(0) - 1)
    def _():
        y_copy.wait()


def write_out(rows, uid, merged, y, dg):
    tokens, hidden = y.shape
    tile = next(t for t in range(160, 0, -8) if rows % t == 0)
    hbm = pl.BlockSpec(memory_space=pl.ANY)
    vm = pl.BlockSpec(memory_space=pltpu.VMEM)
    return pl.pallas_call(
        write_kernel,
        grid=(rows // tile,),
        out_shape=(
            jax.ShapeDtypeStruct((rows, hidden), F32),
            jax.ShapeDtypeStruct((tokens, hidden), BF16),
            jax.ShapeDtypeStruct((1, hidden), F32),
        ),
        in_specs=[pl.BlockSpec(memory_space=pltpu.SMEM), vm, vm, vm],
        out_specs=(pl.BlockSpec((tile, hidden), lambda i: (i, 0)), hbm, vm),
        scratch_shapes=[pltpu.SMEM((1,), jnp.int32), pltpu.SemaphoreType.DMA((1,))],
        compiler_params=pltpu.CompilerParams(vmem_limit_bytes=24 * 1024 * 1024),
        name='write_out',
    )(uid, merged, y, dg)


def short_path(n, rows, uid, kmap, code, send, gain, grad):
    m = n // CORES
    _, tokens, hidden = grad.shape
    vm = pl.BlockSpec(memory_space=pltpu.VMEM)
    hbm = pl.BlockSpec(memory_space=pl.ANY)
    dma = pltpu.SemaphoreType.DMA
    tiles = tokens // TILE
    y, merged, dg = pl.pallas_call(
        functools.partial(core_kernel, n),
        out_shape=(
            jax.ShapeDtypeStruct((tokens, hidden), BF16),
            jax.ShapeDtypeStruct((UNION, hidden), F32),
            jax.ShapeDtypeStruct((1, hidden), F32),
        ),
        in_specs=[vm, vm, vm, vm, hbm],
        out_specs=(vm, vm, vm),
        scratch_shapes=[
            pltpu.VMEM((n * STRIDE, hidden), BF16),
            pltpu.VMEM((CAP, hidden), BF16),
            pltpu.VMEM((tokens, hidden), BF16),
            pltpu.VMEM((CORES * tokens, hidden), BF16),
            pltpu.VMEM((tokens, hidden), F32),
            pltpu.VMEM((tokens, LANES), F32),
            pltpu.VMEM((tokens, CORES * LANES), BF16),
            pltpu.VMEM((m, PARTS, MULTI, hidden // PARTS), F32),
            pltpu.VMEM((m, PARTS, SINGLE, hidden // PARTS), BF16),
            pltpu.VMEM((PARTS, MULTI, hidden // PARTS), F32),
            pltpu.VMEM((PARTS, SINGLE, hidden // PARTS), BF16),
            pltpu.VMEM((m, PARTS, MULTI, hidden // PARTS), F32),
            pltpu.VMEM((m, PARTS, SINGLE, hidden // PARTS), BF16),
            pltpu.VMEM((8, hidden), F32),
            pltpu.VMEM((n, 1, hidden), F32),
            dma((8,)), dma((n + 1,)), dma((2, 2)), dma((2, m)), dma((2, 2, PARTS)), dma((2, 2, PARTS)),
            dma((tiles,)), dma((tiles,)), dma((n,)), dma((n,)), dma((2,)),
        ],
        compiler_params=pltpu.CompilerParams(
            collective_id=0, has_side_effects=True, vmem_limit_bytes=52 * 1024 * 1024),
        name='short_path',
    )(send, code, kmap, gain, grad[0])
    table_grad, y, dg = write_out(rows, uid, merged, y, dg)
    return y[None], table_grad, dg[0]


def exchange_kernel(n, per_dest, src, out, send, recv, local):
    me = lax.axis_index('tp')

    def block(d):
        return src.at[d] if per_dest else src

    barrier(n, me)
    own = pltpu.make_async_copy(block(me), out.at[me], local)
    own.start()
    copies = []
    for k in range(1, n):
        peer = lax.rem(me + k, n)
        copies.append(pltpu.make_async_remote_copy(
            src_ref=block(peer), dst_ref=out.at[me], send_sem=send.at[k], recv_sem=recv.at[k],
            device_id={'tp': peer}, device_id_type=MESH))
        copies[-1].start()
    own.wait()
    for copy in copies:
        copy.wait()


def exchange(n, src, collective_id, per_dest):
    shape = src.shape[1:] if per_dest else src.shape
    hbm = pl.BlockSpec(memory_space=pl.ANY)
    dma = pltpu.SemaphoreType.DMA
    return pl.pallas_call(
        functools.partial(exchange_kernel, n, per_dest),
        out_shape=jax.ShapeDtypeStruct((n, *shape), src.dtype),
        in_specs=[hbm],
        out_specs=hbm,
        scratch_shapes=[dma((n,)), dma((n,)), dma(())],
        compiler_params=pltpu.CompilerParams(collective_id=collective_id, has_side_effects=True),
        name=f'exchange{collective_id}',
    )(src)


def norm_pass(embedded, norm_gain, grad_block):
    hidden_f32 = embedded.astype(F32)
    inv_rms = lax.rsqrt(jnp.mean(hidden_f32 * hidden_f32, axis=-1, keepdims=True) + RMS_EPS)
    x_hat = hidden_f32 * inv_rms
    normed = x_hat.astype(BF16) * norm_gain
    grad_f32 = grad_block.astype(F32)
    gain_part = jnp.sum(grad_f32 * x_hat, axis=(0, 1))
    grad_hat = grad_f32 * norm_gain.astype(F32)
    grad_in = (inv_rms * (grad_hat - x_hat * jnp.mean(grad_hat * x_hat, axis=-1, keepdims=True))).astype(BF16)
    return normed, grad_in, gain_part


def dense_path(n, token_ids, table, gain, grad):
    rows, hidden = table.shape
    tokens = grad.shape[1]
    local_ids = token_ids.reshape(-1) - lax.axis_index('tp') * rows
    owned = (local_ids >= 0) & (local_ids < rows)
    looked_up = jnp.take(table, jnp.where(owned, local_ids, 0), axis=0)
    partial = jnp.where(owned[:, None], looked_up, jnp.zeros((), BF16)).reshape(n, tokens, hidden)
    embedded = jnp.sum(exchange(n, partial, 1, True).astype(F32), axis=0).astype(BF16)
    normed, grad_in, gain_part = norm_pass(embedded[None], gain, grad)
    grad_gain = jnp.sum(exchange(n, gain_part.reshape(-1, LANES), 2, False), axis=0).reshape(-1)
    grad_all = exchange(n, grad_in[0], 3, False).reshape(-1, hidden)
    segments = jnp.where(owned, local_ids, rows)
    table_grad = jax.ops.segment_sum(grad_all.astype(F32), segments, num_segments=rows)
    return normed, table_grad, grad_gain


def device_step(n, token_ids, table, gain, grad):
    uid, kmap, code, send, fits = make_lists(token_ids, table, n)
    return lax.cond(
        fits[0, 0] == 1,
        lambda: short_path(n, table.shape[0], uid, kmap, code, send, gain, grad),
        lambda: dense_path(n, token_ids, table, gain, grad),
    )


def solution(mesh):
    n = mesh.shape['tp']
    return jax.shard_map(
        functools.partial(device_step, n), mesh=mesh,
        in_specs=(P('dp', None), P('tp', None), P(None), P('dp', 'tp', None)),
        out_specs=(P('dp', 'tp', None), P(('dp', 'tp'), None), P('dp')), check_vma=False)
```

time: 148 us -> 113 us (0.76)
  other arithmetic: 23.4 us -> 0 us
  local copies, waits for them, and re-layouts: 22 us -> 2.19 us
  Pallas kernels: 101 us -> 108 us
    scatter-add x1 -> x0, other arithmetic: 21.3 us -> none  [short_path(): jnp.zeros((table.shape[0], hidden), F32).at[take]]
    pallas_call x0 -> x1, Pallas kernels: none -> 18.1 us  [write_out(): pl.pallas_call(write_kernel, grid=(rows // tile,), out_shape=(jax.ShapeDt...]
    pallas_call x1, Pallas kernels: 95 us -> 77.1 us  [short_path(): pl.pallas_call(functools.partial(core_kernel, n), out_shape=(jax.ShapeDty...]
    gather x1 -> x0, local copies, waits for them, and re-layouts: 12.9 us -> none  [short_path(): send = jnp.take(table, take, axis=0, mode='clip').reshape(m, CAP, hidden)]
    pallas_call x1, Pallas kernels: 5.77 us -> 13.2 us  [make_lists(): pl.pallas_call(functools.partial(lists_kernel, n, rows), out_shape=(jax.S...]
    unnamed x3 -> x4, local copies, waits for them, and re-layouts: 5.9 us -> 0.01 us
    cond x0 -> x2, local copies, waits for them, and re-layouts: none -> 2.18 us
    reshape x2 -> x0, local copies, waits for them, and re-layouts: 1.92 us -> none  [the longest x1 1.29 us: short_path(): gain.reshape(1, hidden)]
where the time goes in v2:
time: 113 us; the launch traced here: 112 us
  Pallas kernels  108 us (96%)
  local copies, waits for them, and re-layouts  2.19 us (2%)
  between operations  1.5 us (1%)
    pallas_call x1, Pallas kernels, short_path(): pl.pallas_call(functools.partial(core_kernel, n), out_shape=(jax.ShapeDty...  77.1 us
    pallas_call x1, Pallas kernels, write_out(): pl.pallas_call(write_kernel, grid=(rows // tile,), out_shape=(jax.ShapeDt...  18.1 us
    pallas_call x1, Pallas kernels, make_lists(): pl.pallas_call(functools.partial(lists_kernel, n, rows), out_shape=(jax.S...  13.2 us

profile of v2, /device:TPU:81, one launch (start us, length us, event | category | flops | bytes accessed | tf_op | source)
XLA Modules:
  0.0 112.4 jit_solution(5093097164907716860)
XLA Ops:
  0.6 0.0 copy-start.3
  0.6 0.0 copy-start.2
  0.6 13.2 %lists.1 = (s32[8,256]{1,0:T(8,128)S(1)}, f32[4,256]{1,0:T(4,128)S(1)}, f32[2,2048]{1,0:T(2,128)S(1)}, bf16[4,112,2048]{2,1,0:T(8,128)(2,1)S(1)}, s32[1,1]{1,0:T(1,128)}) custom-call(s32[1,8192]{1,0:T(1,128)} %ids_ref.1, bf16[500,8,2048]{2,1,0:T(8,128)(2,1)} %bitcast.35), custom_call_target="tpu_custom_call" | custom-call | tf_op jit(solution)/shard_map/lists/pallas_call | solution.py:169
  14.5 0.0 copy-done.3
  14.5 0.0 copy-done.2
  14.5 97.6 %conditional.1 = (bf16[1,1024,2048]{2,1,0:T(8,128)(2,1)}, f32[4000,2048]{1,0:T(8,128)}, f32[2048]{0:T(1024)}) conditional(s32[]{:T(128)} %bitcast.14, (s32[1,8192]{1,0:T(1,128)S(1)}, bf16[4000,2048]{1,0:T(8,128)(2,1)}, bf16[2048]{0:T(1024)(128)(2,1)S(1)}, bf16[1,1024,2048]{2,1,0:T(8,128)(2,1)}) %tuple.29, (bf16[1,1024,2048]{2,1,0:T(8,128)(2,1)}, ...), branch_computations={%region_0.7_spmd, %region_7.8_spmd} | conditional | flops 130210816 | bytes 289170016 | solution.py:588
  14.8 77.1 %short_path.1 = (bf16[1024,2048]{1,0:T(8,128)(2,1)}, f32[240,2048]{1,0:T(8,128)S(1)}, f32[1,2048]{1,0:T(1,128)S(1)}) custom-call(bf16[4,112,2048]{2,1,0:T(8,128)(2,1)S(1)} %get-tuple-element.25.rows_ref, f32[2,2048]{1,0:T(2,128)S(1)} %get-tuple-element.26.code_ref, f32[4,256]{1,0:T(4,128)S(1)} %get-tuple-element.27.kmap_ref, ...), custom_call_target="tpu_custom_call" | custom-call | tf_op jit(solution)/shard_map/cond/branch_1_fun/short_path/pallas_call | solution.py:486
  91.9 0.0 copy-start
  91.9 2.2 %copy-done = bf16[1024,2048]{1,0:T(8,128)(2,1)S(1)} copy-done((bf16[1024,2048]{1,0:T(8,128)(2,1)S(1)}, bf16[1024,2048]{1,0:T(8,128)(2,1)}, u32[]{:S(2)}) %copy-start) | copy-done | bytes 4194328 | tf_op jit(solution)/shard_map/cond
  94.1 18.1 %write_out.1 = (f32[4000,2048]{1,0:T(8,128)}, bf16[1024,2048]{1,0:T(8,128)(2,1)}, f32[1,2048]{1,0:T(1,128)}) custom-call(s32[8,256]{1,0:T(8,128)S(1)} %get-tuple-element.24.uid_s, f32[240,2048]{1,0:T(8,128)S(1)} %get-tuple-element.30.merged_ref, bf16[1024,2048]{1,0:T(8,128)(2,1)S(1)} %copy-done, f32[1,2048]{1,0:T(1,128)S(1)} %get-tuple-element.32.dg_ref), custom_call_target="tpu_custom_call" | custom-call | tf_op jit(solution)/shard_map/cond/branch_1_fun/write_out/pallas_call | solution.py:463
Async XLA Ops:
  0.6 13.9 %copy-start.3 = (bf16[2048]{0:T(1024)(128)(2,1)S(1)}, bf16[2048]{0:T(1024)(128)(2,1)}, u32[]{:S(2)}) copy-start(bf16[2048]{0:T(1024)(128)(2,1)} %param.8) | copy-start | bytes 12292
  0.6 13.9 %copy-start.2 = (s32[1,8192]{1,0:T(1,128)S(1)}, s32[1,8192]{1,0:T(1,128)}, u32[]{:S(2)}) copy-start(s32[1,8192]{1,0:T(1,128)} %ids_ref.1) | copy-start | bytes 98308
  91.9 2.2 %copy-start = (bf16[1024,2048]{1,0:T(8,128)(2,1)S(1)}, bf16[1024,2048]{1,0:T(8,128)(2,1)}, u32[]{:S(2)}) copy-start(bf16[1024,2048]{1,0:T(8,128)(2,1)} %get-tuple-element.31.y_ref) | copy-start | bytes 12582916 | tf_op jit(solution)/shard_map/cond

commit v3 on v2

--- a/solution.py
+++ b/solution.py
@@ -157,8 +157,11 @@
         return carry
 
     lax.fori_loop(0, groups, pick, 0)
-    for j in range(m):
-        send_ref[j] = jnp.dot(spread[j], picked[...], preferred_element_type=F32).astype(BF16)
+    spread = jnp.concatenate(spread, axis=0)
+    for c in range(0, table.shape[2], CODE):
+        rows_out = jnp.dot(spread, picked[:, c:c + CODE], preferred_element_type=F32).astype(BF16)
+        for j in range(m):
+            send_ref[j, :, c:c + CODE] = rows_out[j * CAP:(j + 1) * CAP]
 
 
 def make_lists(token_ids, table, n):
@@ -198,8 +201,8 @@
     pl.semaphore_wait(sem, n - 1)
 
 
-def core_kernel(n, rows_ref, code_ref, kmap_ref, gain_ref, dy_hbm, y, merged, dg_ref,
-                got, relay, dy, dx, xs, codes, pick_x, psum, pone, rsum, rone, gsum, gone, dgacc, dgs,
+def core_kernel(n, rows_ref, code_ref, kmap_ref, gain_ref, dy_hbm, y_hbm, merged, dg_ref,
+                got, relay, dy, y, dx, xs, codes, pick_x, psum, pone, rsum, rone, gsum, gone, dgacc, dgs,
                 fsend, frecv, bsend, brecv, psend, precv, tsend, trecv, gsend, grecv, local):
     m = n // CORES
     tokens, hidden = dy_hbm.shape
@@ -331,6 +334,8 @@
         return carry
 
     lax.fori_loop(0, tiles, norm_tile, 0)
+    y_copy = pltpu.make_async_copy(y, y_hbm, local.at[2])
+    y_copy.start()
 
     dgs[me] = jnp.sum(dgacc[...], axis=0, keepdims=True)
     for k in range(1, n):
@@ -427,51 +432,68 @@
     merge(far, gsum.at[far], gone.at[far], False)
     for copy in (to_far, to_behind, to_ahead, to_sib, passed, *shared, *first, *direct, *relays):
         copy.wait_send()
-
-
-def write_kernel(uid_s, merged_ref, y_ref, dg_ref, table_grad_ref, y_out, dg_out, at, sem):
-    step, tile = pl.program_id(0), table_grad_ref.shape[0]
-    y_copy = pltpu.make_async_copy(y_ref, y_out, sem.at[0])
-
-    @pl.when(step == 0)
-    def _():
-        y_copy.start()
-        dg_out[...] = dg_ref[...]
-        at[0] = 0
-
-    table_grad_ref[...] = jnp.zeros_like(table_grad_ref)
-
-    def more(p):
-        return uid_s[0, p] < (step + 1) * tile
-
-    def put(p):
-        table_grad_ref[pl.ds(uid_s[0, p] - step * tile, 1), :] = merged_ref[pl.ds(p, 1), :]
-        return p + 1
-
-    at[0] = lax.while_loop(more, put, at[0])
-
-    @pl.when(step == pl.num_programs(0) - 1)
-    def _():
-        y_copy.wait()
+    y_copy.wait()
+
+
+def write_kernel(uid_s, merged_ref, y_hbm, dg_ref, out, y_out, dg_out, y, buffers, sem, sem_y):
+    slots, tile, _ = buffers.shape
+    steps = out.shape[0] // tile
+    y_in = pltpu.make_async_copy(y_hbm, y, sem_y.at[0])
+    y_back = pltpu.make_async_copy(y, y_out, sem_y.at[1])
+    y_in.start()
+    dg_out[...] = dg_ref[...]
+
+    def send(i):
+        slot = lax.rem(i, slots)
+        rows = pl.ds(pl.multiple_of(i * tile, tile), tile)
+        return pltpu.make_async_copy(buffers.at[slot], out.at[rows], sem.at[slot])
+
+    def fill(i, p):
+        slot = lax.rem(i, slots)
+
+        @pl.when(i >= slots)
+        def _():
+            send(i - slots).wait()
+
+        buffers[slot] = jnp.zeros(buffers.shape[1:], F32)
+
+        def put(p):
+            buffers[slot, pl.ds(uid_s[0, p] - i * tile, 1), :] = merged_ref[pl.ds(p, 1), :]
+            return p + 1
+
+        p = lax.while_loop(lambda p: uid_s[0, p] < (i + 1) * tile, put, p)
+        send(i).start()
+        return p
+
+    p = lax.fori_loop(0, slots, fill, 0)
+    y_in.wait()
+    y_back.start()
+    lax.fori_loop(slots, steps, fill, p)
+    for i in range(steps - slots, steps):
+        send(i).wait()
+    y_back.wait()
 
 
 def write_out(rows, uid, merged, y, dg):
     tokens, hidden = y.shape
     tile = next(t for t in range(160, 0, -8) if rows % t == 0)
+    slots = min(8, rows // tile)
     hbm = pl.BlockSpec(memory_space=pl.ANY)
     vm = pl.BlockSpec(memory_space=pltpu.VMEM)
     return pl.pallas_call(
         write_kernel,
-        grid=(rows // tile,),
         out_shape=(
             jax.ShapeDtypeStruct((rows, hidden), F32),
             jax.ShapeDtypeStruct((tokens, hidden), BF16),
             jax.ShapeDtypeStruct((1, hidden), F32),
         ),
-        in_specs=[pl.BlockSpec(memory_space=pltpu.SMEM), vm, vm, vm],
-        out_specs=(pl.BlockSpec((tile, hidden), lambda i: (i, 0)), hbm, vm),
-        scratch_shapes=[pltpu.SMEM((1,), jnp.int32), pltpu.SemaphoreType.DMA((1,))],
-        compiler_params=pltpu.CompilerParams(vmem_limit_bytes=24 * 1024 * 1024),
+        in_specs=[pl.BlockSpec(memory_space=pltpu.SMEM), vm, hbm, vm],
+        out_specs=(hbm, hbm, vm),
+        scratch_shapes=[
+            pltpu.VMEM((tokens, hidden), BF16), pltpu.VMEM((slots, tile, hidden), F32),
+            pltpu.SemaphoreType.DMA((slots,)), pltpu.SemaphoreType.DMA((2,)),
+        ],
+        compiler_params=pltpu.CompilerParams(vmem_limit_bytes=60 * 1024 * 1024),
         name='write_out',
     )(uid, merged, y, dg)
 
@@ -491,10 +513,11 @@
             jax.ShapeDtypeStruct((1, hidden), F32),
         ),
         in_specs=[vm, vm, vm, vm, hbm],
-        out_specs=(vm, vm, vm),
+        out_specs=(hbm, vm, vm),
         scratch_shapes=[
             pltpu.VMEM((n * STRIDE, hidden), BF16),
             pltpu.VMEM((CAP, hidden), BF16),
+            pltpu.VMEM((tokens, hidden), BF16),
             pltpu.VMEM((tokens, hidden), BF16),
             pltpu.VMEM((CORES * tokens, hidden), BF16),
             pltpu.VMEM((tokens, hidden), F32),
@@ -509,7 +532,7 @@
             pltpu.VMEM((8, hidden), F32),
             pltpu.VMEM((n, 1, hidden), F32),
             dma((8,)), dma((n + 1,)), dma((2, 2)), dma((2, m)), dma((2, 2, PARTS)), dma((2, 2, PARTS)),
-            dma((tiles,)), dma((tiles,)), dma((n,)), dma((n,)), dma((2,)),
+            dma((tiles,)), dma((tiles,)), dma((n,)), dma((n,)), dma((3,)),
         ],
         compiler_params=pltpu.CompilerParams(
             collective_id=0, has_side_effects=True, vmem_limit_bytes=52 * 1024 * 1024),

time: 113 us -> 108 us (0.956)
  Pallas kernels: 108 us -> 104 us
    pallas_call x1, Pallas kernels: 18.1 us -> 15.8 us  [write_out(): pl.pallas_call(write_kernel, out_shape=(jax.ShapeDtypeStruct((rows, hidde...]
    pallas_call x1, Pallas kernels: 77.1 us -> 75.7 us  [short_path(): pl.pallas_call(functools.partial(core_kernel, n), out_shape=(jax.ShapeDty...]
where the time goes in v3:
time: 108 us
  Pallas kernels  104 us (96%)
  local copies, waits for them, and re-layouts  1.9 us (2%)
  between operations  1.5 us (1%)
    pallas_call x1, Pallas kernels, short_path(): pl.pallas_call(functools.partial(core_kernel, n), out_shape=(jax.ShapeDty...  75.7 us
    pallas_call x1, Pallas kernels, write_out(): pl.pallas_call(write_kernel, out_shape=(jax.ShapeDtypeStruct((rows, hidde...  15.8 us
    pallas_call x1, Pallas kernels, make_lists(): pl.pallas_call(functools.partial(lists_kernel, n, rows), out_shape=(jax.S...  13 us

profile of v3, /device:TPU:81, one launch (start us, length us, event | category | flops | bytes accessed | tf_op | source)
XLA Modules:
  0.0 108.1 jit_solution(16791068067948414600)
XLA Ops:
  0.6 0.0 copy-start.4
  0.6 0.0 copy-start.3
  0.6 13.0 %lists.1 = (s32[8,256]{1,0:T(8,128)S(1)}, f32[4,256]{1,0:T(4,128)S(1)}, f32[2,2048]{1,0:T(2,128)S(1)}, bf16[4,112,2048]{2,1,0:T(8,128)(2,1)S(1)}, s32[1,1]{1,0:T(1,128)}) custom-call(s32[1,8192]{1,0:T(1,128)} %ids_ref.1, bf16[500,8,2048]{2,1,0:T(8,128)(2,1)} %bitcast.35), custom_call_target="tpu_custom_call" | custom-call | tf_op jit(solution)/shard_map/lists/pallas_call | solution.py:172
  14.3 0.0 copy-done.4
  14.3 0.0 copy-done.3
  14.3 93.6 %conditional.1 = (bf16[1,1024,2048]{2,1,0:T(8,128)(2,1)}, f32[4000,2048]{1,0:T(8,128)}, f32[2048]{0:T(1024)}) conditional(s32[]{:T(128)} %bitcast.14, (s32[1,8192]{1,0:T(1,128)S(1)}, bf16[4000,2048]{1,0:T(8,128)(2,1)}, bf16[2048]{0:T(1024)(128)(2,1)S(1)}, bf16[1,1024,2048]{2,1,0:T(8,128)(2,1)}) %tuple.29, (bf16[1,1024,2048]{2,1,0:T(8,128)(2,1)}, ...), branch_computations={%region_0.7_spmd, %region_7.8_spmd} | conditional | flops 130210816 | bytes 289170016 | solution.py:611
  14.5 75.7 %short_path.1 = (bf16[1024,2048]{1,0:T(8,128)(2,1)}, f32[240,2048]{1,0:T(8,128)S(1)}, f32[1,2048]{1,0:T(1,128)S(1)}) custom-call(bf16[4,112,2048]{2,1,0:T(8,128)(2,1)S(1)} %get-tuple-element.25.rows_ref, f32[2,2048]{1,0:T(2,128)S(1)} %get-tuple-element.26.code_ref, f32[4,256]{1,0:T(4,128)S(1)} %get-tuple-element.27.kmap_ref, ...), custom_call_target="tpu_custom_call" | custom-call | tf_op jit(solution)/shard_map/cond/branch_1_fun/short_path/pallas_call | solution.py:508
  90.2 0.0 copy-start
  90.3 1.3 %copy-done = f32[240,2048]{1,0:T(8,128)} copy-done((f32[240,2048]{1,0:T(8,128)}, f32[240,2048]{1,0:T(8,128)S(1)}, u32[]{:S(2)}) %copy-start) | copy-done | bytes 1966104 | tf_op jit(solution)/shard_map/cond
  91.5 0.0 copy-start.1
  91.5 0.6 copy-done.1
  92.1 15.8 %write_out.1 = (f32[4000,2048]{1,0:T(8,128)}, bf16[1024,2048]{1,0:T(8,128)(2,1)}, f32[1,2048]{1,0:T(1,128)}) custom-call(s32[8,256]{1,0:T(8,128)S(1)} %get-tuple-element.24.uid_s, f32[240,2048]{1,0:T(8,128)} %copy-done, bf16[1024,2048]{1,0:T(8,128)(2,1)} %get-tuple-element.31.y_hbm, f32[1,2048]{1,0:T(1,128)} %copy-done.1), custom_call_target="tpu_custom_call" | custom-call | tf_op jit(solution)/shard_map/cond/branch_1_fun/write_out/pallas_call | solution.py:483
Async XLA Ops:
  0.6 13.7 %copy-start.4 = (bf16[2048]{0:T(1024)(128)(2,1)S(1)}, bf16[2048]{0:T(1024)(128)(2,1)}, u32[]{:S(2)}) copy-start(bf16[2048]{0:T(1024)(128)(2,1)} %param.8) | copy-start | bytes 12292
  0.6 13.7 %copy-start.3 = (s32[1,8192]{1,0:T(1,128)S(1)}, s32[1,8192]{1,0:T(1,128)}, u32[]{:S(2)}) copy-start(s32[1,8192]{1,0:T(1,128)} %ids_ref.1) | copy-start | bytes 98308
  90.2 1.3 %copy-start = (f32[240,2048]{1,0:T(8,128)}, f32[240,2048]{1,0:T(8,128)S(1)}, u32[]{:S(2)}) copy-start(f32[240,2048]{1,0:T(8,128)S(1)} %get-tuple-element.30.merged_ref) | copy-start | bytes 5898244 | tf_op jit(solution)/shard_map/cond
  91.5 0.6 copy-start.1

commit v4 on v3

--- a/solution.py
+++ b/solution.py
@@ -201,8 +201,8 @@
     pl.semaphore_wait(sem, n - 1)
 
 
-def core_kernel(n, rows_ref, code_ref, kmap_ref, gain_ref, dy_hbm, y_hbm, merged, dg_ref,
-                got, relay, dy, y, dx, xs, codes, pick_x, psum, pone, rsum, rone, gsum, gone, dgacc, dgs,
+def core_kernel(n, rows_ref, code_ref, kmap_ref, gain_ref, dy_hbm, y, merged, dg_ref,
+                got, relay, dy, dx, xs, codes, pick_x, psum, pone, rsum, rone, gsum, gone, dgacc, dgs,
                 fsend, frecv, bsend, brecv, psend, precv, tsend, trecv, gsend, grecv, local):
     m = n // CORES
     tokens, hidden = dy_hbm.shape
@@ -334,8 +334,6 @@
         return carry
 
     lax.fori_loop(0, tiles, norm_tile, 0)
-    y_copy = pltpu.make_async_copy(y, y_hbm, local.at[2])
-    y_copy.start()
 
     dgs[me] = jnp.sum(dgacc[...], axis=0, keepdims=True)
     for k in range(1, n):
@@ -432,15 +430,13 @@
     merge(far, gsum.at[far], gone.at[far], False)
     for copy in (to_far, to_behind, to_ahead, to_sib, passed, *shared, *first, *direct, *relays):
         copy.wait_send()
-    y_copy.wait()
-
-
-def write_kernel(uid_s, merged_ref, y_hbm, dg_ref, out, y_out, dg_out, y, buffers, sem, sem_y):
+
+
+def write_kernel(uid_s, merged_ref, y, dg_ref, out, y_out, dg_out, buffers, sem, sem_y):
     slots, tile, _ = buffers.shape
     steps = out.shape[0] // tile
-    y_in = pltpu.make_async_copy(y_hbm, y, sem_y.at[0])
-    y_back = pltpu.make_async_copy(y, y_out, sem_y.at[1])
-    y_in.start()
+    y_back = pltpu.make_async_copy(y, y_out, sem_y)
+    y_back.start()
     dg_out[...] = dg_ref[...]
 
     def send(i):
@@ -465,10 +461,7 @@
         send(i).start()
         return p
 
-    p = lax.fori_loop(0, slots, fill, 0)
-    y_in.wait()
-    y_back.start()
-    lax.fori_loop(slots, steps, fill, p)
+    lax.fori_loop(0, steps, fill, 0)
     for i in range(steps - slots, steps):
         send(i).wait()
     y_back.wait()
@@ -487,13 +480,12 @@
             jax.ShapeDtypeStruct((tokens, hidden), BF16),
             jax.ShapeDtypeStruct((1, hidden), F32),
         ),
-        in_specs=[pl.BlockSpec(memory_space=pltpu.SMEM), vm, hbm, vm],
+        in_specs=[pl.BlockSpec(memory_space=pltpu.SMEM), vm, vm, vm],
         out_specs=(hbm, hbm, vm),
         scratch_shapes=[
-            pltpu.VMEM((tokens, hidden), BF16), pltpu.VMEM((slots, tile, hidden), F32),
-            pltpu.SemaphoreType.DMA((slots,)), pltpu.SemaphoreType.DMA((2,)),
+            pltpu.VMEM((slots, tile, hidden), F32), pltpu.SemaphoreType.DMA((slots,)), pltpu.SemaphoreType.DMA(()),
         ],
-        compiler_params=pltpu.CompilerParams(vmem_limit_bytes=60 * 1024 * 1024),
+        compiler_params=pltpu.CompilerParams(vmem_limit_bytes=24 * 1024 * 1024),
         name='write_out',
     )(uid, merged, y, dg)
 
@@ -513,11 +505,10 @@
             jax.ShapeDtypeStruct((1, hidden), F32),
         ),
         in_specs=[vm, vm, vm, vm, hbm],
-        out_specs=(hbm, vm, vm),
+        out_specs=(vm, vm, vm),
         scratch_shapes=[
             pltpu.VMEM((n * STRIDE, hidden), BF16),
             pltpu.VMEM((CAP, hidden), BF16),
-            pltpu.VMEM((tokens, hidden), BF16),
             pltpu.VMEM((tokens, hidden), BF16),
             pltpu.VMEM((CORES * tokens, hidden), BF16),
             pltpu.VMEM((tokens, hidden), F32),
@@ -532,10 +523,10 @@
             pltpu.VMEM((8, hidden), F32),
             pltpu.VMEM((n, 1, hidden), F32),
             dma((8,)), dma((n + 1,)), dma((2, 2)), dma((2, m)), dma((2, 2, PARTS)), dma((2, 2, PARTS)),
-            dma((tiles,)), dma((tiles,)), dma((n,)), dma((n,)), dma((3,)),
+            dma((tiles,)), dma((tiles,)), dma((n,)), dma((n,)), dma((2,)),
         ],
         compiler_params=pltpu.CompilerParams(
-            collective_id=0, has_side_effects=True, vmem_limit_bytes=52 * 1024 * 1024),
+            collective_id=0, has_side_effects=True, vmem_limit_bytes=44 * 1024 * 1024),
         name='short_path',
     )(send, code, kmap, gain, grad[0])
     table_grad, y, dg = write_out(rows, uid, merged, y, dg)

time: 108 us -> 104 us (0.963)
  Pallas kernels: 104 us -> 102 us
  local copies, waits for them, and re-layouts: 1.9 us -> 0.01 us
    pallas_call x1, Pallas kernels: 15.8 us -> 13.2 us  [write_out(): pl.pallas_call(write_kernel, out_shape=(jax.ShapeDtypeStruct((rows, hidde...]
    cond x4 -> x0, local copies, waits for them, and re-layouts: 1.89 us -> none
where the time goes in v4:
time: 104 us; the launch traced here: 103 us
  Pallas kernels  102 us (98%)
  between operations  1.5 us (1%)
    pallas_call x1, Pallas kernels, short_path(): pl.pallas_call(functools.partial(core_kernel, n), out_shape=(jax.ShapeDty...  75.5 us
    pallas_call x1, Pallas kernels, write_out(): pl.pallas_call(write_kernel, out_shape=(jax.ShapeDtypeStruct((rows, hidde...  13.2 us
    pallas_call x1, Pallas kernels, make_lists(): pl.pallas_call(functools.partial(lists_kernel, n, rows), out_shape=(jax.S...  13 us

profile of v4, /device:TPU:81, one launch (start us, length us, event | category | flops | bytes accessed | tf_op | source)
XLA Modules:
  0.0 103.5 jit_solution(4851314923443785324)
XLA Ops:
  0.6 0.0 copy-start.2
  0.6 0.0 copy-start.1
  0.6 13.0 %lists.1 = (s32[8,256]{1,0:T(8,128)S(1)}, f32[4,256]{1,0:T(4,128)S(1)}, f32[2,2048]{1,0:T(2,128)S(1)}, bf16[4,112,2048]{2,1,0:T(8,128)(2,1)S(1)}, s32[1,1]{1,0:T(1,128)}) custom-call(s32[1,8192]{1,0:T(1,128)} %ids_ref.1, bf16[500,8,2048]{2,1,0:T(8,128)(2,1)} %bitcast.35), custom_call_target="tpu_custom_call" | custom-call | tf_op jit(solution)/shard_map/lists/pallas_call | solution.py:172
  14.3 0.0 copy-done.2
  14.3 0.0 copy-done.1
  14.3 89.0 %conditional.1 = (bf16[1,1024,2048]{2,1,0:T(8,128)(2,1)}, f32[4000,2048]{1,0:T(8,128)}, f32[2048]{0:T(1024)}) conditional(s32[]{:T(128)} %bitcast.14, (s32[1,8192]{1,0:T(1,128)S(1)}, bf16[4000,2048]{1,0:T(8,128)(2,1)}, bf16[2048]{0:T(1024)(128)(2,1)S(1)}, bf16[1,1024,2048]{2,1,0:T(8,128)(2,1)}) %tuple.29, (bf16[1,1024,2048]{2,1,0:T(8,128)(2,1)}, ...), branch_computations={%region_0.7_spmd, %region_7.8_spmd} | conditional | flops 130210816 | bytes 289170016 | solution.py:602
  14.5 75.5 %short_path.1 = (bf16[1024,2048]{1,0:T(8,128)(2,1)S(1)}, f32[240,2048]{1,0:T(8,128)S(1)}, f32[1,2048]{1,0:T(1,128)S(1)}) custom-call(bf16[4,112,2048]{2,1,0:T(8,128)(2,1)S(1)} %get-tuple-element.25.rows_ref, f32[2,2048]{1,0:T(2,128)S(1)} %get-tuple-element.26.code_ref, f32[4,256]{1,0:T(4,128)S(1)} %get-tuple-element.27.kmap_ref, ...), custom_call_target="tpu_custom_call" | custom-call | tf_op jit(solution)/shard_map/cond/branch_1_fun/short_path/pallas_call | solution.py:500
  90.1 13.2 %write_out.1 = (f32[4000,2048]{1,0:T(8,128)}, bf16[1024,2048]{1,0:T(8,128)(2,1)}, f32[1,2048]{1,0:T(1,128)}) custom-call(s32[8,256]{1,0:T(8,128)S(1)} %get-tuple-element.24.uid_s, f32[240,2048]{1,0:T(8,128)S(1)} %get-tuple-element.30.merged_ref, bf16[1024,2048]{1,0:T(8,128)(2,1)S(1)} %get-tuple-element.31.y, f32[1,2048]{1,0:T(1,128)S(1)} %get-tuple-element.32.dg_ref), custom_call_target="tpu_custom_call" | custom-call | tf_op jit(solution)/shard_map/cond/branch_1_fun/write_out/pallas_call | solution.py:476
Async XLA Ops:
  0.6 13.7 %copy-start.2 = (bf16[2048]{0:T(1024)(128)(2,1)S(1)}, bf16[2048]{0:T(1024)(128)(2,1)}, u32[]{:S(2)}) copy-start(bf16[2048]{0:T(1024)(128)(2,1)} %param.8) | copy-start | bytes 12292
  0.6 13.7 %copy-start.1 = (s32[1,8192]{1,0:T(1,128)S(1)}, s32[1,8192]{1,0:T(1,128)}, u32[]{:S(2)}) copy-start(s32[1,8192]{1,0:T(1,128)} %ids_ref.1) | copy-start | bytes 98308
